TPU v7x, 32 devices: a whole 2x2x4 slice. The times are simulated.
32 devices in a mesh: t: 4 (over z), v: 8 (over y, x, core).
Axes of the slice: x: 2, y: 2, z: 4, core: 2. Of those that a mesh axis runs over, the one named last changes fastest.
Arguments:
- hidden_in: bfloat16 [1024, 2304], replicated
- seq_lens: int32 [1024], replicated
- target: int32 [1024], replicated
- g_attn_pre: bfloat16 [2304], replicated
- w_q: bfloat16 [2304, 2048], P(None, 't')
- w_k: bfloat16 [2304, 1024], P(None, 't')
- w_v: bfloat16 [2304, 1024], P(None, 't')
- w_o: bfloat16 [2048, 2304], P('t')
- g_attn_post: bfloat16 [2304], replicated
- g_mlp_pre: bfloat16 [2304], replicated
- w_gate: bfloat16 [2304, 9216], P(None, 't')
- w_up: bfloat16 [2304, 9216], P(None, 't')
- w_down: bfloat16 [9216, 2304], P('t')
- g_mlp_post: bfloat16 [2304], replicated
- g_final: bfloat16 [2304], replicated
- k_cache: bfloat16 [1024, 32, 4, 256], P(None, None, 't')
- v_cache: bfloat16 [1024, 32, 4, 256], P(None, None, 't')
- embed_table: bfloat16 [256000, 2304], P(('v', 't'))
Outputs:
- output 1: float32 [1024], replicated
- output 2: bfloat16 [1024, 2304], replicated
All inputs are finite; a program needn't handle non-finite values.
Results may differ from a plain program's by a relative error of at most 0.0078882.
Values sent between devices are 32-bit elements.
A program may use at most 1 GiB of HBM per device.

v0:
```python
import jax
import jax.numpy as jnp
from jax import lax
from jax.sharding import PartitionSpec as P

ATTN_CAP = 50.0
FINAL_CAP = 30.0
NORM_EPS = 1e-6
ROPE_BASE = 10000.0


def rms_norm(values, gain_vec):
    x_f32 = values.astype(jnp.float32)
    scaled = x_f32 * lax.rsqrt(jnp.mean(x_f32 * x_f32, axis=-1, keepdims=True) + NORM_EPS)
    return scaled * (1.0 + gain_vec.astype(jnp.float32))


def rotary(values, positions):
    half_dim = values.shape[-1] // 2
    inv_freq = ROPE_BASE ** (-2.0 * jnp.arange(half_dim, dtype=jnp.float32) / values.shape[-1])
    angles = positions.astype(jnp.float32)[:, None] * inv_freq[None, :]
    angles = angles.reshape((values.shape[0],) + (1,) * (values.ndim - 2) + (half_dim,))
    cos_t = jnp.cos(angles)
    sin_t = jnp.sin(angles)
    x_low = values[..., :half_dim]
    x_high = values[..., half_dim:]
    return jnp.concatenate([x_low * cos_t - x_high * sin_t, x_high * cos_t + x_low * sin_t], axis=-1)


def attention(normed, seq_lens, w_q, w_k, w_v, k_cache, v_cache):
    tokens, ctx_len, kv_heads, head_dim = k_cache.shape
    group_size = w_q.shape[1] // (kv_heads * head_dim)
    score_scale = head_dim ** -0.5
    q_rot = rotary(jnp.dot(normed, w_q, preferred_element_type=jnp.float32).reshape(tokens, kv_heads, group_size, head_dim), seq_lens).astype(jnp.bfloat16)
    k_rot = rotary(jnp.dot(normed, w_k, preferred_element_type=jnp.float32).reshape(tokens, kv_heads, head_dim), seq_lens).astype(jnp.bfloat16)
    v_new = jnp.dot(normed, w_v, preferred_element_type=jnp.float32).astype(jnp.bfloat16).reshape(tokens, kv_heads, head_dim)
    s_cache = jnp.einsum('nkgd,ntkd->nkgt', q_rot, k_cache, preferred_element_type=jnp.float32) * score_scale
    s_new = jnp.einsum('nkgd,nkd->nkg', q_rot, k_rot, preferred_element_type=jnp.float32) * score_scale
    s_cache = ATTN_CAP * jnp.tanh(s_cache / ATTN_CAP)
    s_new = ATTN_CAP * jnp.tanh(s_new / ATTN_CAP)
    valid_mask = jnp.arange(ctx_len)[None, :] < seq_lens[:, None]
    s_cache = jnp.where(valid_mask[:, None, None, :], s_cache, -1e30)
    row_max = jnp.maximum(jnp.max(s_cache, axis=-1), s_new)
    p_cache = jnp.exp(s_cache - row_max[..., None])
    p_new = jnp.exp(s_new - row_max)
    denominator = jnp.sum(p_cache, axis=-1) + p_new
    weighted = jnp.einsum('nkgt,ntkd->nkgd', p_cache.astype(jnp.bfloat16), v_cache, preferred_element_type=jnp.float32)
    weighted = weighted + p_new.astype(jnp.bfloat16).astype(jnp.float32)[..., None] * v_new.astype(jnp.float32)[:, :, None, :]
    return (weighted / denominator[..., None]).astype(jnp.bfloat16).reshape(tokens, kv_heads * group_size * head_dim)


def solution(mesh):
    tp_size = mesh.shape['t']
    in_specs = (P(), P(), P(), P(), P(None, 't'), P(None, 't'), P(None, 't'), P('t', None), P(), P(), P(None, 't'), P(None, 't'), P('t', None), P(), P(), P(None, None, 't', None), P(None, None, 't', None), P(('v', 't'), None))

    def local_step(hidden_in, seq_lens, target, g_attn_pre, w_q, w_k, w_v, w_o, g_attn_post, g_mlp_pre, w_gate, w_up, w_down, g_mlp_post, g_final, k_cache, v_cache, embed_table):
        normed = rms_norm(hidden_in, g_attn_pre).astype(jnp.bfloat16)
        attn_vec = attention(normed, seq_lens, w_q, w_k, w_v, k_cache, v_cache)
        attn_part = jnp.dot(attn_vec, w_o, preferred_element_type=jnp.float32)
        attn_out = lax.psum(attn_part, 't')
        hidden_mid = (hidden_in.astype(jnp.float32) + rms_norm(attn_out, g_attn_post)).astype(jnp.bfloat16)
        mlp_in = rms_norm(hidden_mid, g_mlp_pre).astype(jnp.bfloat16)
        gate_proj = jnp.dot(mlp_in, w_gate, preferred_element_type=jnp.float32)
        up_proj = jnp.dot(mlp_in, w_up, preferred_element_type=jnp.float32)
        activated = (jax.nn.gelu(gate_proj, approximate=True) * up_proj).astype(jnp.bfloat16)
        mlp_part = jnp.dot(activated, w_down, preferred_element_type=jnp.float32)
        mlp_out = lax.psum(mlp_part, 't')
        hidden_out = (hidden_mid.astype(jnp.float32) + rms_norm(mlp_out, g_mlp_post)).astype(jnp.bfloat16)
        final_h = rms_norm(hidden_out, g_final).astype(jnp.bfloat16)
        logits = lax.dot_general(final_h, embed_table, (((1,), (1,)), ((), ())), preferred_element_type=jnp.float32)
        capped = FINAL_CAP * jnp.tanh(logits / FINAL_CAP)
        vocab_local = embed_table.shape[0]
        shard_index = lax.axis_index('v') * tp_size + lax.axis_index('t')
        row_ids = shard_index * vocab_local + jnp.arange(vocab_local)
        local_max = jnp.max(capped, axis=1)
        local_sum = jnp.sum(jnp.exp(capped - local_max[:, None]), axis=1)
        local_tgt = jnp.sum(jnp.where(row_ids[None, :] == target[:, None], capped, 0.0), axis=1)
        gathered = lax.all_gather(jnp.stack([local_max, local_sum, local_tgt]), ('v', 't'))
        glob_max = jnp.max(gathered[:, 0], axis=0)
        glob_sum = jnp.sum(gathered[:, 1] * jnp.exp(gathered[:, 0] - glob_max[None, :]), axis=0)
        logprob = jnp.sum(gathered[:, 2], axis=0) - glob_max - jnp.log(glob_sum)
        return logprob, hidden_out

    return jax.shard_map(local_step, mesh=mesh, in_specs=in_specs, out_specs=(P(), P()), check_vma=False)
```

profile of v0, /device:TPU:0, one launch (start us, length us, event | category | flops | bytes accessed | tf_op | source)
XLA Modules:
  0.0 954.3 jit_solution(1304901358330428475)
XLA Ops:
  10.2 3.3 fusion.8
  13.5 5.7 fusion.80
  20.3 2.3 copy.46
  23.9 4.4 convolution_bitcast_fusion
  28.3 3.1 multiply_cosine_fusion.1
  31.4 2.3 fusion.68
  36.3 2.5 fusion.65
  39.8 3.1 multiply_reduce_fusion.2
  44.1 9.2 fusion.85
  53.8 15.5 %fusion.57 = f32[1024,2]{1,0:T(8,128)S(1)} fusion(f32[1024,2,32]{2,1,0:T(2,128)} %get-tuple-element.23, f32[1024,2]{1,0:T(8,128)S(1)} %copy.35), kind=kLoop, calls=%fused_computation.70 | loop fusion | flops 129024 | bytes 278528 | tf_op jit(solution)/shard_map/reduce_sum | solution.py:46
  70.8 4.3 fusion.39
  75.1 8.2 fusion.34
  83.6 5.1 fusion.86
  88.7 325.4 %all-reduce.3.cloned.1.call-done = f32[1024,2304]{1,0:T(8,128)} async-done(((f32[1024,2304]{1,0:T(8,128)}), f32[1024,2304]{1,0:T(8,128)}) %all-reduce.3.cloned.1.call-update) | async-done | bytes 9437200 | tf_op jit(solution)/shard_map/psum | solution.py:60
  414.1 4.4 multiply_reduce_fusion.1
  418.5 6.3 fusion.12
  427.1 15.7 %fusion.37 = f32[1024,2304]{1,0:T(8,128)} fusion(bf16[2304,2304]{1,0:T(8,128)(2,1)} %param.28, bf16[1024,2304]{1,0:T(8,128)(2,1)S(1)} %get-tuple-element.9, f32[2304]{0:T(1024)S(1)} %convert_add_fusion.4, f32[1024]{0:T(1024)S(1)} %add_rsqrt_fusion.2), kind=kOutput, calls=%fused_computation.51 | convolution fusion | flops 10881073152 | bytes 24785920 | tf_op jit(solution)/shard_map/dot_general | solution.py:63
  442.7 35.0 %fusion.25 = f32[1024,2304]{1,0:T(8,128)} fusion(bf16[2304,2304]{1,0:T(8,128)(2,1)} %param.30, f32[1024,2304]{1,0:T(8,128)} %fusion.37, bf16[2304,2304]{1,0:T(8,128)(2,1)} %param.29, bf16[1024,2304]{1,0:T(8,128)(2,1)} %copy-done.2, f32[2304]{0:T(1024)S(1)} %convert_add_fusion.4, f32[1024]{0:T(1024)S(1)} %add_rsqrt_fusion.2), kind=kOutput, calls=%fused_computation.39 | convolution fusion | flops 21776302080 | bytes 44839936 | tf_op jit(solution)/shard_map/dot_general | solution.py:66
  478.5 321.0 %all-reduce.5.cloned.1.call-done = f32[1024,2304]{1,0:T(8,128)} async-done(((f32[1024,2304]{1,0:T(8,128)}), f32[1024,2304]{1,0:T(8,128)}) %all-reduce.5.cloned.1.call-update) | async-done | bytes 9437200 | tf_op jit(solution)/shard_map/psum | solution.py:67
  799.5 4.4 multiply_reduce_fusion
  803.9 6.3 fusion.5
  810.3 49.2 %fusion = (f32[1024]{0:T(1024)S(1)}, f32[1024,8000]{0,1:T(8,128)}) fusion(bf16[8000,2304]{1,0:T(8,128)(2,1)} %param.35, bf16[1024,2304]{1,0:T(8,128)(2,1)S(1)} %get-tuple-element.7, f32[2304]{0:T(1024)S(1)} %convert_add_fusion.2, f32[1024]{0:T(1024)S(1)} %add_rsqrt_fusion), kind=kOutput, calls=%fused_computation.3 | convolution fusion | flops 37782749184 | bytes 74368000 | tf_op jit(solution)/shard_map/dot_general | solution.py:70
  859.4 16.6 %exponential_reduce_fusion = (f32[1024]{0:T(1024)S(1)}, f32[1024]{0:T(1024)S(1)}) fusion(f32[1024,8000]{0,1:T(8,128)} %get-tuple-element.25, f32[1024]{0:T(1024)S(1)} %get-tuple-element.24, s32[1024]{0:T(1024)S(1)} %copy-done.13, s32[8000]{0:T(1024)S(1)} %iota_add_fusion), kind=kLoop, calls=%fused_computation.1 | loop fusion | flops 57341952 | bytes 32816384 | tf_op jit(solution)/shard_map/reduce_sum | solution.py:76
  876.0 70.0 %all-gather.1 = f32[32,3,1024]{2,1,0:T(4,128)S(1)} all-gather(f32[1,3,1024]{2,1,0:T(4,128)S(1)} %maximum_bitcast_fusion), channel_id=2, replica_groups=mesh['t'=4,'v'=8] {'v','t'}, dimensions={0}, use_global_device_ids=true | all-gather | bytes 405504 | tf_op jit(solution)/shard_map/all_gather | solution.py:78
  (69 shorter events, 16.4 us)
Async XLA Ops:
  7.2 76.4 %copy-start = (bf16[512,2304]{1,0:T(8,128)(2,1)S(1)}, bf16[512,2304]{1,0:T(8,128)(2,1)}, u32[]{:S(2)}) copy-start(bf16[512,2304]{1,0:T(8,128)(2,1)} %param.25) | copy-start | bytes 7077892
  7.2 407.0 %all-reduce.3.cloned.1.call-start = ((), (), s32[]{:S(2)}) async-start(), calls=%async_computation | async-start | bytes 18874368 | tf_op jit(solution)/shard_map/psum | solution.py:60
  10.2 13.8 %copy-start.8 = (f32[2304]{0:T(1024)}, f32[2304]{0:T(1024)S(1)}, u32[]{:S(2)}) copy-start(f32[2304]{0:T(1024)S(1)} %convert_add_fusion.6) | copy-start | bytes 27652
  13.5 5.7 copy-start.14
  23.9 4.4 copy-start.16
  38.8 0.8 copy-start.4
  38.8 1.0 copy-start.5
  44.1 26.7 %copy-start.15 = (f32[1024]{0:T(1024)S(1)}, f32[1024]{0:T(1024)}, u32[]{:S(2)}) copy-start(f32[1024]{0:T(1024)} %copy-done.14) | copy-start | bytes 12292
  70.8 4.3 copy-start.6
  70.8 4.3 copy-start.7
  83.5 5.2 copy-start.9
  83.5 5.2 copy-start.10
  88.6 710.8 %all-reduce.5.cloned.1.call-start = ((), (), s32[]{:S(2)}) async-start(), calls=%async_computation.1 | async-start | bytes 18874368 | tf_op jit(solution)/shard_map/psum | solution.py:67
  424.9 2.2 copy-start.2
  477.8 0.7 copy-start.11
  477.8 0.7 copy-start.12
  810.2 49.2 %copy-start.3 = (bf16[1024,2304]{1,0:T(8,128)(2,1)}, bf16[1024,2304]{1,0:T(8,128)(2,1)S(1)}, u32[]{:S(2)}) copy-start(bf16[1024,2304]{1,0:T(8,128)(2,1)S(1)} %get-tuple-element.7) | copy-start | bytes 14155780
  810.2 49.2 %copy-start.13 = (s32[1024]{0:T(1024)S(1)}, s32[1024]{0:T(1024)}, u32[]{:S(2)}) copy-start(s32[1024]{0:T(1024)} %param.20) | copy-start | bytes 12292
  859.4 87.7 %copy-start.1 = (bf16[512,2304]{1,0:T(8,128)(2,1)S(1)}, bf16[512,2304]{1,0:T(8,128)(2,1)}, u32[]{:S(2)}) copy-start(bf16[512,2304]{1,0:T(8,128)(2,1)} %param.25) | copy-start | bytes 7077892
Sparse Core Ops, SparseCore 0:
  88.8 325.3 all-reduce.2
  477.9 321.5 all-reduce.4
where the time goes:
time: 963 us; the launch traced here: 954 us
  waiting for transfers between devices  646 us (67%)
  matrix products  137 us (14%)
  other arithmetic  72.9 us (8%)
  blocking collectives  70 us (7%)
  between operations  14.8 us (2%)
  local copies, waits for them, and re-layouts  13.4 us (1%)
    psum x1, waiting for transfers between devices, local_step(): attn_out = lax.psum(attn_part, 't')  325 us
    psum x1, waiting for transfers between devices, local_step(): mlp_out = lax.psum(mlp_part, 't')  321 us
    all_gather x1, blocking collectives, local_step(): lax.all_gather(jnp.stack([local_max, local_sum, local_tgt]), ('v', 't'))  70 us
    dot_general x1, matrix products, local_step(): lax.dot_general(final_h, embed_table, (((1,), (1,)), ((), ())), preferred...  49.2 us
    dot_general x1, matrix products, local_step(): mlp_part = jnp.dot(activated, w_down, preferred_element_type=jnp.float32)  35 us
    reduce_sum x5, other arithmetic, rms_norm(): jnp.mean(x_f32 * x_f32, axis=-1, keepdims=True) + NORM_EPS  24.8 us
  transfers between devices with their start and end apart: 2, of which 2 were waited for; matrix products, arithmetic and copies ran while one was open for 0% of the time, Pallas kernels for 0%

commit v1 on v0

--- a/solution.py
+++ b/solution.py
@@ -1,12 +1,19 @@
+import functools
+import math
+
 import jax
 import jax.numpy as jnp
 from jax import lax
+from jax.experimental import pallas as pl
+from jax.experimental.pallas import tpu as pltpu
 from jax.sharding import PartitionSpec as P
 
 ATTN_CAP = 50.0
 FINAL_CAP = 30.0
 NORM_EPS = 1e-6
 ROPE_BASE = 10000.0
+MESH = pl.DeviceIdType.MESH
+VMEM_LIMIT = 66_000_000
 
 
 def rms_norm(values, gain_vec):
@@ -49,36 +56,329 @@
     return (weighted / denominator[..., None]).astype(jnp.bfloat16).reshape(tokens, kv_heads * group_size * head_dim)
 
 
+def line_reduce_kernel(chunks, lag, part_ref, res_ref, gain_ref, out_ref, sum_buf, end_buf, mate_buf, res_buf, send_sem, recv_sem):
+    t = lax.axis_index('t')
+    rows = part_ref.shape[0] // chunks
+    is_end = t * (3 - t) == 0
+    inner = 1 + t // 3
+    outer = 3 * (t - 1)
+    mate = 3 - t
+    barrier = pltpu.get_barrier_semaphore()
+
+    def piece(ref, c):
+        return ref.at[pl.ds(c * rows, rows)]
+
+    def copy(src, dst, stage, c, to):
+        return pltpu.make_async_remote_copy(
+            src_ref=piece(src, c), dst_ref=piece(dst, c), send_sem=send_sem.at[stage, c],
+            recv_sem=recv_sem.at[stage, c], device_id={'t': to}, device_id_type=MESH)
+
+    @pl.when(is_end)
+    def _():
+        pl.semaphore_signal(barrier, inc=1, device_id={'t': inner}, device_id_type=MESH)
+        pl.semaphore_wait(barrier, 1)
+        for c in range(chunks):
+            copy(part_ref, end_buf, 0, c, inner).start()
+        for c in range(chunks):
+            copy(res_buf, res_buf, 2, c, inner).wait_recv()
+            piece(out_ref, c)[...] = piece(res_buf, c)[...].astype(out_ref.dtype)
+        for c in range(chunks):
+            copy(part_ref, end_buf, 0, c, inner).wait_send()
+
+    @pl.when(jnp.logical_not(is_end))
+    def _():
+        pl.semaphore_signal(barrier, inc=1, device_id={'t': outer}, device_id_type=MESH)
+        pl.semaphore_signal(barrier, inc=1, device_id={'t': mate}, device_id_type=MESH)
+        pl.semaphore_wait(barrier, 2)
+        for i in range(chunks + lag):
+            if i < chunks:
+                copy(part_ref, end_buf, 0, i, outer).wait_recv()
+                piece(sum_buf, i)[...] = piece(part_ref, i)[...] + piece(end_buf, i)[...]
+                copy(sum_buf, mate_buf, 1, i, mate).start()
+            j = i - lag
+            if j >= 0:
+                copy(sum_buf, mate_buf, 1, j, mate).wait_recv()
+                total = piece(sum_buf, j)[...] + piece(mate_buf, j)[...]
+                scaled = total * lax.rsqrt(jnp.mean(total * total, axis=-1, keepdims=True) + NORM_EPS)
+                done = (piece(res_ref, j)[...].astype(jnp.float32) + scaled * gain_ref[...]).astype(jnp.bfloat16)
+                piece(res_buf, j)[...] = done.astype(jnp.float32)
+                piece(out_ref, j)[...] = done.astype(out_ref.dtype)
+                copy(res_buf, res_buf, 2, j, outer).start()
+        for c in range(chunks):
+            copy(sum_buf, mate_buf, 1, c, mate).wait_send()
+            copy(res_buf, res_buf, 2, c, outer).wait_send()
+
+
+def line_reduce(part, residual, gain, out_dtype, collective_id, chunks=8, lag=2):
+    rows, width = part.shape
+    return pl.pallas_call(
+        functools.partial(line_reduce_kernel, chunks, lag),
+        out_shape=jax.ShapeDtypeStruct((rows, width), out_dtype),
+        in_specs=[pl.BlockSpec(memory_space=pltpu.VMEM)] * 3,
+        out_specs=pl.BlockSpec(memory_space=pltpu.VMEM),
+        scratch_shapes=[pltpu.VMEM((rows, width), jnp.float32)] * 4 + [pltpu.SemaphoreType.DMA((3, chunks))] * 2,
+        compiler_params=pltpu.CompilerParams(collective_id=collective_id, has_side_effects=True),
+        cost_estimate=pl.CostEstimate(flops=60_000_000_000, bytes_accessed=4 * rows * width, transcendentals=0),
+        name=f'line_reduce_{collective_id}',
+    )(part, residual, 1.0 + gain.astype(jnp.float32)[None, :])
+
+
+def head_kernel(tiles, y_in, gain_ref, tgt_ref, e_hbm, lp_ref, y_ref, e_buf, gath, h_buf, log_a, log_b, acc_s, acc_t,
+                stat, plane_stat, part_stat, line_stat, e_sem, own_send, fwd_send, unit_recv, st_send, st_recv, ln_send, ln_recv):
+    v = lax.axis_index('v')
+    t = lax.axis_index('t')
+    vy, vx, vc = v // 4, (v // 2) % 2, v % 2
+    units, unit_rows, width = gath.shape
+    row_tile = e_buf.shape[0] // tiles
+    group = 4 * unit_rows
+
+    def block(yf, xf, cf):
+        return (vy + yf) % 2 * 4 + (vx + xf) % 2 * 2 + (vc + cf) % 2
+
+    here, pair, near_x, near_y = block(0, 0, 0), block(0, 0, 1), block(0, 1, 0), block(1, 0, 0)
+
+    def tile_copy(k):
+        part = pl.ds(k * row_tile, row_tile)
+        return pltpu.make_async_copy(e_hbm.at[part], e_buf.at[part], e_sem.at[k])
+
+    def fetch(k, carry):
+        tile_copy(k).start()
+        return carry
+
+    lax.fori_loop(0, tiles, fetch, 0)
+
+    barrier = pltpu.get_barrier_semaphore()
+    for d in range(1, 8):
+        pl.semaphore_signal(barrier, inc=1, device_id={'v': (v + d) % 8}, device_id_type=MESH)
+    for d in range(1, 4):
+        pl.semaphore_signal(barrier, inc=1, device_id={'t': (t + d) % 4}, device_id_type=MESH)
+    pl.semaphore_wait(barrier, 10)
+
+    def own_copy(h, i, to):
+        return pltpu.make_async_remote_copy(
+            src_ref=y_in.at[h], dst_ref=gath.at[2 * here + h], send_sem=own_send.at[h, i],
+            recv_sem=unit_recv.at[2 * here + h], device_id={'v': to}, device_id_type=MESH)
+
+    def forward(u, i, to):
+        return pltpu.make_async_remote_copy(
+            src_ref=gath.at[u], dst_ref=gath.at[u], send_sem=fwd_send.at[i],
+            recv_sem=unit_recv.at[u], device_id={'v': to}, device_id_type=MESH)
+
+    def arrived(u):
+        pltpu.make_async_remote_copy(
+            src_ref=gath.at[u], dst_ref=gath.at[u], send_sem=fwd_send.at[0],
+            recv_sem=unit_recv.at[u], device_id={'v': pair}, device_id_type=MESH).wait_recv()
+
+    for h in range(2):
+        own_copy(h, 0, near_x).start()
+        own_copy(h, 1, near_y).start()
+        own_copy(h, 2, pair).start()
+    for h in range(2):
+        gath[2 * here + h] = y_in[h]
+
+    def unit_of(g, q):
+        mid = jnp.logical_or(g == 1, g == 2)
+        half = jnp.where(mid, g - 1, q % 2)
+        xf = jnp.where(mid, 1 - q % 2, g // 3)
+        yf = jnp.where(mid, q % 2, g // 3)
+        return 2 * block(yf, xf, q // 2) + half
+
+    def far(yf, xf, cf, h):
+        return 2 * block(yf, xf, cf) + h
+
+    first_row = (v * 4 + t) * e_buf.shape[0]
+    sub_rows = row_tile // 10 if (row_tile // 10) % 8 == 0 else row_tile
+
+    def group_step(g, carry):
+        @pl.when(g == 0)
+        def _():
+            for h in range(2):
+                arrived(far(0, 0, 1, h))
+
+        for k in range(2):
+            @pl.when(g == 1 + k)
+            def _():
+                ux, uy = far(0, 1, 0, k), far(1, 0, 0, k)
+                arrived(ux)
+                if k == 0:
+                    forward(ux, 0, near_y).start()
+                forward(ux, 2 + k, pair).start()
+                arrived(uy)
+                if k == 1:
+                    forward(uy, 1, near_x).start()
+                forward(uy, 4 + k, pair).start()
+                arrived(far(0, 1, 1, k))
+                arrived(far(1, 0, 1, k))
+
+        @pl.when(g == 3)
+        def _():
+            for h in range(2):
+                arrived(far(1, 1, 0, h))
+                forward(far(1, 1, 0, h), 6 + h, pair).start()
+            for h in range(2):
+                arrived(far(1, 1, 1, h))
+
+        lanes = []
+        for q in range(4):
+            u = unit_of(g, q)
+            y = gath[u]
+            y_ref[u] = y.astype(jnp.bfloat16)
+            h = y * lax.rsqrt(jnp.mean(y * y, axis=-1, keepdims=True) + NORM_EPS) * gain_ref[...]
+            h_buf[q * unit_rows:(q + 1) * unit_rows, :] = h.astype(jnp.bfloat16)
+            lanes.append(tgt_ref[pl.ds(u, 1), :])
+        local_tgt = jnp.concatenate(lanes, axis=1) - first_row
+        acc_s[...] = jnp.zeros_like(acc_s)
+        acc_t[...] = jnp.zeros_like(acc_t)
+
+        def logits(r, dst):
+            @pl.when(g == 0)
+            def _():
+                tile_copy(r).wait()
+            start = pl.multiple_of(r * row_tile, row_tile)
+            dst[...] = lax.dot_general(e_buf[pl.ds(start, row_tile), :], h_buf[...], (((1,), (1,)), ((), ())), preferred_element_type=jnp.float32)
+
+        def reduce_tile(r, src):
+            total_s, total_t = acc_s[...], acc_t[...]
+            sub = lax.broadcasted_iota(jnp.int32, (sub_rows, group), 0)
+            for p in range(row_tile // sub_rows):
+                capped = jnp.tanh(src[p * sub_rows:(p + 1) * sub_rows, :] * (1.0 / FINAL_CAP))
+                hit = sub == local_tgt - (r * row_tile + p * sub_rows)
+                powers = jnp.exp2(capped * (FINAL_CAP * math.log2(math.e)))
+                total_s = total_s + jnp.sum(powers.reshape(sub_rows // 8, 8, group), axis=0)
+                total_t = total_t + jnp.sum(jnp.where(hit, capped, 0.0).reshape(sub_rows // 8, 8, group), axis=0)
+            acc_s[...] = total_s
+            acc_t[...] = total_t
+
+        logits(0, log_a)
+
+        def pair_step(i, c):
+            logits(2 * i + 1, log_b)
+            reduce_tile(2 * i, log_a)
+            logits(2 * i + 2, log_a)
+            reduce_tile(2 * i + 1, log_b)
+            return c
+
+        lax.fori_loop(0, tiles // 2 - 1, pair_step, 0)
+        logits(tiles - 1, log_b)
+        reduce_tile(tiles - 2, log_a)
+        reduce_tile(tiles - 1, log_b)
+
+        sums = jnp.sum(acc_s[...], axis=0, keepdims=True)
+        hits = jnp.sum(acc_t[...], axis=0, keepdims=True) * FINAL_CAP
+        for q in range(4):
+            u = unit_of(g, q)
+            stat[0, pl.ds(u, 1), :] = sums[:, q * unit_rows:(q + 1) * unit_rows]
+            stat[1, pl.ds(u, 1), :] = hits[:, q * unit_rows:(q + 1) * unit_rows]
+        return carry
+
+    lax.fori_loop(0, 4, group_step, 0)
+
+    def plane_copy(d):
+        return pltpu.make_async_remote_copy(
+            src_ref=stat, dst_ref=plane_stat.at[v], send_sem=st_send.at[d - 1],
+            recv_sem=st_recv.at[v], device_id={'v': (v + d) % 8}, device_id_type=MESH)
+
+    def plane_wait(d):
+        other = (v + d) % 8
+        pltpu.make_async_remote_copy(
+            src_ref=stat, dst_ref=plane_stat.at[other], send_sem=st_send.at[d - 1],
+            recv_sem=st_recv.at[other], device_id={'v': other}, device_id_type=MESH).wait_recv()
+
+    def line_copy(d):
+        return pltpu.make_async_remote_copy(
+            src_ref=part_stat, dst_ref=line_stat.at[t], send_sem=ln_send.at[d - 1],
+            recv_sem=ln_recv.at[t], device_id={'t': (t + d) % 4}, device_id_type=MESH)
+
+    def line_wait(d):
+        other = (t + d) % 4
+        pltpu.make_async_remote_copy(
+            src_ref=part_stat, dst_ref=line_stat.at[other], send_sem=ln_send.at[d - 1],
+            recv_sem=ln_recv.at[other], device_id={'t': other}, device_id_type=MESH).wait_recv()
+
+    for d in range(1, 8):
+        plane_copy(d).start()
+    plane_stat[v] = stat[...]
+    for d in range(1, 8):
+        plane_wait(d)
+    part_stat[...] = jnp.sum(plane_stat[...], axis=0)
+    for d in range(1, 4):
+        line_copy(d).start()
+    line_stat[t] = part_stat[...]
+    for d in range(1, 4):
+        line_wait(d)
+    final = line_stat[0] + line_stat[1] + line_stat[2] + line_stat[3]
+    lp_ref[...] = final[1] - jnp.log(final[0])
+
+    for h in range(2):
+        for i, to in enumerate((near_x, near_y, pair)):
+            own_copy(h, i, to).wait_send()
+    forward(far(0, 1, 0, 0), 0, near_y).wait_send()
+    forward(far(1, 0, 0, 1), 1, near_x).wait_send()
+    for k in range(2):
+        forward(far(0, 1, 0, k), 2 + k, pair).wait_send()
+        forward(far(1, 0, 0, k), 4 + k, pair).wait_send()
+        forward(far(1, 1, 0, k), 6 + k, pair).wait_send()
+    for d in range(1, 8):
+        plane_copy(d).wait_send()
+    for d in range(1, 4):
+        line_copy(d).wait_send()
+
+
+def gather_and_head(y_block, gain, target, embed_table, collective_id, tiles=10):
+    rows, width = y_block.shape
+    unit_rows = rows // 2
+    vocab_local = embed_table.shape[0]
+    row_tile = vocab_local // tiles
+    dma = pltpu.SemaphoreType.DMA
+    stat_shape = (2, 16, unit_rows)
+    logprob, hidden_out = pl.pallas_call(
+        functools.partial(head_kernel, tiles),
+        out_shape=(jax.ShapeDtypeStruct((16, unit_rows), jnp.float32), jax.ShapeDtypeStruct((16, unit_rows, width), jnp.bfloat16)),
+        in_specs=[pl.BlockSpec(memory_space=pltpu.VMEM)] * 3 + [pl.BlockSpec(memory_space=pl.ANY)],
+        out_specs=(pl.BlockSpec(memory_space=pltpu.VMEM), pl.BlockSpec(memory_space=pltpu.VMEM)),
+        scratch_shapes=[
+            pltpu.VMEM((vocab_local, width), jnp.bfloat16),
+            pltpu.VMEM((16, unit_rows, width), jnp.float32),
+            pltpu.VMEM((4 * unit_rows, width), jnp.bfloat16),
+            pltpu.VMEM((row_tile, 4 * unit_rows), jnp.float32),
+            pltpu.VMEM((row_tile, 4 * unit_rows), jnp.float32),
+            pltpu.VMEM((8, 4 * unit_rows), jnp.float32),
+            pltpu.VMEM((8, 4 * unit_rows), jnp.float32),
+            pltpu.VMEM(stat_shape, jnp.float32),
+            pltpu.VMEM((8,) + stat_shape, jnp.float32),
+            pltpu.VMEM(stat_shape, jnp.float32),
+            pltpu.VMEM((4,) + stat_shape, jnp.float32),
+            dma((tiles,)), dma((2, 3)), dma((8,)), dma((16,)), dma((7,)), dma((8,)), dma((3,)), dma((4,)),
+        ],
+        compiler_params=pltpu.CompilerParams(collective_id=collective_id, has_side_effects=True, vmem_limit_bytes=VMEM_LIMIT),
+        cost_estimate=pl.CostEstimate(flops=2 * 8 * rows * width * vocab_local, bytes_accessed=2 * vocab_local * width, transcendentals=2 * 8 * rows * vocab_local),
+        name='gather_and_head',
+    )(y_block.reshape(2, unit_rows, width), 1.0 + gain.astype(jnp.float32)[None, :], target.reshape(16, unit_rows), embed_table)
+    return logprob.reshape(8 * rows), hidden_out.reshape(8 * rows, width)
+
+
 def solution(mesh):
-    tp_size = mesh.shape['t']
+    v_size = mesh.shape['v']
     in_specs = (P(), P(), P(), P(), P(None, 't'), P(None, 't'), P(None, 't'), P('t', None), P(), P(), P(None, 't'), P(None, 't'), P('t', None), P(), P(), P(None, None, 't', None), P(None, None, 't', None), P(('v', 't'), None))
 
     def local_step(hidden_in, seq_lens, target, g_attn_pre, w_q, w_k, w_v, w_o, g_attn_post, g_mlp_pre, w_gate, w_up, w_down, g_mlp_post, g_final, k_cache, v_cache, embed_table):
-        normed = rms_norm(hidden_in, g_attn_pre).astype(jnp.bfloat16)
-        attn_vec = attention(normed, seq_lens, w_q, w_k, w_v, k_cache, v_cache)
+        rows = hidden_in.shape[0] // v_size
+        start = lax.axis_index('v') * rows
+
+        def mine(array):
+            return lax.dynamic_slice_in_dim(array, start, rows, 0)
+
+        x, lens = mine(hidden_in), mine(seq_lens)
+        normed = rms_norm(x, g_attn_pre).astype(jnp.bfloat16)
+        attn_vec = attention(normed, lens, w_q, w_k, w_v, mine(k_cache), mine(v_cache))
         attn_part = jnp.dot(attn_vec, w_o, preferred_element_type=jnp.float32)
-        attn_out = lax.psum(attn_part, 't')
-        hidden_mid = (hidden_in.astype(jnp.float32) + rms_norm(attn_out, g_attn_post)).astype(jnp.bfloat16)
+        hidden_mid = line_reduce(attn_part, x, g_attn_post, jnp.bfloat16, 0)
         mlp_in = rms_norm(hidden_mid, g_mlp_pre).astype(jnp.bfloat16)
         gate_proj = jnp.dot(mlp_in, w_gate, preferred_element_type=jnp.float32)
         up_proj = jnp.dot(mlp_in, w_up, preferred_element_type=jnp.float32)
         activated = (jax.nn.gelu(gate_proj, approximate=True) * up_proj).astype(jnp.bfloat16)
         mlp_part = jnp.dot(activated, w_down, preferred_element_type=jnp.float32)
-        mlp_out = lax.psum(mlp_part, 't')
-        hidden_out = (hidden_mid.astype(jnp.float32) + rms_norm(mlp_out, g_mlp_post)).astype(jnp.bfloat16)
-        final_h = rms_norm(hidden_out, g_final).astype(jnp.bfloat16)
-        logits = lax.dot_general(final_h, embed_table, (((1,), (1,)), ((), ())), preferred_element_type=jnp.float32)
-        capped = FINAL_CAP * jnp.tanh(logits / FINAL_CAP)
-        vocab_local = embed_table.shape[0]
-        shard_index = lax.axis_index('v') * tp_size + lax.axis_index('t')
-        row_ids = shard_index * vocab_local + jnp.arange(vocab_local)
-        local_max = jnp.max(capped, axis=1)
-        local_sum = jnp.sum(jnp.exp(capped - local_max[:, None]), axis=1)
-        local_tgt = jnp.sum(jnp.where(row_ids[None, :] == target[:, None], capped, 0.0), axis=1)
-        gathered = lax.all_gather(jnp.stack([local_max, local_sum, local_tgt]), ('v', 't'))
-        glob_max = jnp.max(gathered[:, 0], axis=0)
-        glob_sum = jnp.sum(gathered[:, 1] * jnp.exp(gathered[:, 0] - glob_max[None, :]), axis=0)
-        logprob = jnp.sum(gathered[:, 2], axis=0) - glob_max - jnp.log(glob_sum)
-        return logprob, hidden_out
+        y_block = line_reduce(mlp_part, hidden_mid, g_mlp_post, jnp.float32, 1)
+        return gather_and_head(y_block, g_final, target, embed_table, 2)
 
     return jax.shard_map(local_step, mesh=mesh, in_specs=in_specs, out_specs=(P(), P()), check_vma=False)

time: 963 us -> 234 us (0.24)
  waiting for transfers between devices: 646 us -> 0 us
  Pallas kernels: 0 us -> 189 us
  matrix products: 137 us -> 24.8 us
  blocking collectives: 70 us -> 0 us
  other arithmetic: 72.9 us -> 8.24 us
  between operations: 14.8 us -> 0.88 us
    psum x2 -> x0, waiting for transfers between devices: 646 us -> none  [the longest x1 325 us: local_step(): attn_out = lax.psum(attn_part, 't')]
    pallas_call x0 -> x3, Pallas kernels: none -> 189 us  [the longest x1 104 us: gather_and_head(): pl.pallas_call(functools.partial(head_kernel, tiles), out_shape=(jax.Shap...]
    all_gather x1 -> x0, blocking collectives: 70 us -> none  [local_step(): lax.all_gather(jnp.stack([local_max, local_sum, local_tgt]), ('v', 't'))]
    dot_general x1, matrix products: 49.2 us -> 0.27 us  [attention(): jnp.einsum('nkgd,nkd->nkg', q_rot, k_rot, preferred_element_type=jnp.floa...]
    dot_general x1, matrix products: 35 us -> 11.5 us  [local_step(): mlp_part = jnp.dot(activated, w_down, preferred_element_type=jnp.float32)]
    reduce_sum x5 -> x2, other arithmetic: 24.8 us -> 2.6 us  [rms_norm(): jnp.mean(x_f32 * x_f32, axis=-1, keepdims=True) + NORM_EPS]
    reduce_sum x3 -> x0, other arithmetic: 17 us -> none  [the longest x1 16.6 us: local_step(): local_sum = jnp.sum(jnp.exp(capped - local_max[:, None]), axis=1)]
    reduce_sum x1, other arithmetic: 15.5 us -> 0.39 us  [attention(): denominator = jnp.sum(p_cache, axis=-1) + p_new]
  transfers between devices with their start and end apart: 2 -> 0, of which waited for: 2 -> 0; matrix products, arithmetic and copies ran while one was open for 0% -> 0% of each run, Pallas kernels for 0% -> 0%
where the time goes in v1:
time: 234 us
  Pallas kernels  189 us (81%)
  matrix products  24.8 us (11%)
  local copies, waits for them, and re-layouts  11.2 us (5%)
  other arithmetic  8.24 us (4%)
    pallas_call x1, Pallas kernels, gather_and_head(): pl.pallas_call(functools.partial(head_kernel, tiles), out_shape=(jax.Shap...  104 us
    pallas_call x2, Pallas kernels, line_reduce(): pl.pallas_call(functools.partial(line_reduce_kernel, chunks, lag), out_sh...  84.7 us
    dot_general x1, matrix products, local_step(): mlp_part = jnp.dot(activated, w_down, preferred_element_type=jnp.float32)  11.5 us
    unnamed x14, local copies, waits for them, and re-layouts  6 us
    dot_general x1, matrix products, local_step(): gate_proj = jnp.dot(mlp_in, w_gate, preferred_element_type=jnp.float32)  5.61 us

profile of v1, /device:TPU:0, one launch (start us, length us, event | category | flops | bytes accessed | tf_op | source)
XLA Modules:
  0.0 233.7 jit_solution(103979454226093756)
XLA Ops:
  0.7 0.9 fusion.83
  1.5 1.4 reshape.297.tgt_ref
  2.9 0.7 convert_add_fusion.4
  3.6 0.7 convert_add_fusion.2
  4.3 0.7 convert_add_fusion.3
  5.0 0.6 add.74.gain_ref
  5.6 0.7 convert_add_fusion.1
  6.3 0.6 add.81.gain_ref
  6.9 0.7 convert_add_fusion
  7.6 0.6 add.83.gain_ref
  8.6 1.3 fusion.7
  10.6 0.7 copy-done.5
  12.1 0.5 fusion.81
  13.3 2.4 %fusion.84 = (f32[128,2]{1,0:T(8,128)S(1)}, f32[128,2,32]{2,1,0:T(2,128)S(1)}) fusion(bf16[1024,32,1,256]{3,1,2,0:T(8,128)(2,1)} %param.33, s32[]{:T(128)S(6)} %select_n.11, bf16[128,2,128]{2,1,0:T(2,128)(2,1)S(1)} %get-tuple-element.11, bf16[128,2,128]{2,1,0:T(2,128)(2,1)S(1)} %get-tuple-element.10, pred[128,32]{1,0:T(8,128)(4,1)S(1)} %iota_compare_fusion), kind=kOutput, calls=%fused_computation.93 | convolution fusion | flops 4488960 | bytes 2266116 | tf_op jit(solution)/shard_map/nkgd,ntkd->nkgt/dot_general | solution.py:44
  16.6 2.3 fusion.26
  19.0 1.5 fusion.85.part_ref
  20.5 44.2 %line_reduce_0.1.res_ref = bf16[128,2304]{1,0:T(8,128)(2,1)} custom-call(f32[128,2304]{1,0:T(8,128)} %fusion.85.part_ref, bf16[128,2304]{1,0:T(8,128)(2,1)} %copy-done.3, f32[1,2304]{1,0:T(1,128)} %add.74.gain_ref), custom_call_target="tpu_custom_call" | custom-call | flops 60000002048 | bytes 1179648 | tf_op jit(solution)/shard_map/line_reduce_0/pallas_call | solution.py:114
  64.7 1.3 fusion.10
  66.1 5.6 %fusion.49 = f32[128,2304]{1,0:T(8,128)S(1)} fusion(bf16[2304,2304]{1,0:T(8,128)(2,1)} %param.28, bf16[128,2304]{1,0:T(8,128)(2,1)S(1)} %copy-done, f32[2304]{0:T(1024)S(1)} %convert_add_fusion.2, f32[128]{0:T(128)S(1)} %add_rsqrt_fusion), kind=kOutput, calls=%fused_computation.41 | convolution fusion | flops 1360134144 | bytes 12396032 | tf_op jit(solution)/shard_map/dot_general | solution.py:377
  71.7 11.5 %fusion.42.part_ref = f32[128,2304]{1,0:T(8,128)} fusion(bf16[2304,2304]{1,0:T(8,128)(2,1)} %param.30, bf16[2304,2304]{1,0:T(8,128)(2,1)} %param.29, f32[128,2304]{1,0:T(8,128)S(1)} %fusion.49, bf16[128,2304]{1,0:T(8,128)(2,1)S(1)} %copy-done, f32[2304]{0:T(1024)S(1)} %convert_add_fusion.2, f32[128]{0:T(128)S(1)} %add_rsqrt_fusion), kind=kOutput, calls=%fused_computation.36 | convolution fusion | flops 2722037760 | bytes 24192512 | tf_op jit(solution)/shard_map/dot_general | solution.py:380
  83.2 40.5 %line_reduce_1.1 = f32[128,2304]{1,0:T(8,128)} custom-call(f32[128,2304]{1,0:T(8,128)} %fusion.42.part_ref, bf16[128,2304]{1,0:T(8,128)(2,1)} %line_reduce_0.1.res_ref, f32[1,2304]{1,0:T(1,128)} %add.81.gain_ref), custom_call_target="tpu_custom_call" | custom-call | flops 60000002048 | bytes 1179648 | tf_op jit(solution)/shard_map/line_reduce_1/pallas_call | solution.py:114
  123.7 103.9 %gather_and_head.1 = (f32[16,64]{1,0:T(8,128)}, bf16[16,64,2304]{2,1,0:T(8,128)(2,1)}) custom-call(f32[2,64,2304]{2,1,0:T(8,128)} %bitcast.67, f32[1,2304]{1,0:T(1,128)} %add.83.gain_ref, s32[16,64]{1,0:T(8,128)} %reshape.297.tgt_ref, bf16[8000,2304]{1,0:T(8,128)(2,1)} %e_hbm.1), custom_call_target="tpu_custom_call" | custom-call | flops 37748736000 | bytes 36864000 | tf_op jit(solution)/shard_map/gather_and_head/pallas_call | solution.py:334
  227.6 1.4 reshape.298
  228.9 4.8 %copy.34 = bf16[1024,2304]{1,0:T(8,128)(2,1)} copy(bf16[1024,2304]{1,0:T(8,128)(2,1)} %bitcast.64) | data formatting | bytes 9437184
  (33 shorter events, 3.5 us)
Async XLA Ops:
  0.6 9.2 %copy-start.4 = (bf16[2304,256]{1,0:T(8,128)(2,1)S(1)}, bf16[2304,256]{1,0:T(8,128)(2,1)}, u32[]{:S(2)}) copy-start(bf16[2304,256]{1,0:T(8,128)(2,1)} %param.23) | copy-start | bytes 3538948
  9.8 1.9 copy-start.3
  9.9 1.5 copy-start.5
  10.2 1.9 copy-start.1
  16.6 2.4 %copy-start.2 = (bf16[512,2304]{1,0:T(8,128)(2,1)S(1)}, bf16[512,2304]{1,0:T(8,128)(2,1)}, u32[]{:S(2)}) copy-start(bf16[512,2304]{1,0:T(8,128)(2,1)} %param.25) | copy-start | bytes 7077892
  64.7 1.3 copy-start
